TPU v7x, 32 devices: a whole 2x2x4 slice. The times are simulated.
32 devices in a mesh: depth: 2 (over core), rows: 4 (over y, x), cols: 4 (over z).
Axes of the slice: x: 2, y: 2, z: 4, core: 2. Of those that a mesh axis runs over, the one named last changes fastest.
Arguments:
- section_states: float32 [2, 128, 64, 256], P('depth', 'rows', 'cols'), may hold values from -6 to 6
- weights: bfloat16 [4, 3, 3, 256, 256], P('depth'), may hold values from -0.125 to 0.125
Outputs:
- fine_states: float32 [4, 128, 64, 256], P('depth', 'rows', 'cols')
- coarse_states: float32 [2, 128, 64, 256], P('depth', 'rows', 'cols')
All inputs are finite; a program needn't handle non-finite values.
Results may differ from a plain program's by a relative error of at most 0.002.
Values may be sent and summed in bfloat16 or wider, within the bound.
A program may use at most 64 MiB of HBM per device.

v0:
```python
import jax
import jax.numpy as jnp
from jax import lax
from jax.sharding import PartitionSpec as P


def padded_2(shard, sides, width):
    for axis, dim in sides:
        size, length = (lax.axis_size(axis), shard.shape[dim])
        up = [(i, (i + 1) % size) for i in range(size - 1)]
        down = [(j, i) for i, j in up]
        last = lax.slice_in_dim(shard, length - width, length, axis=dim)
        initial = lax.slice_in_dim(shard, 0, width, axis=dim)
        before = lax.ppermute(last, axis, up)
        after = lax.ppermute(initial, axis, down)
        shard = jnp.concatenate([before, shard, after], axis=dim)
    return shard


def shifted_2(block, axis, distance):
    devices = range(lax.axis_size(axis))
    route = [(i - distance, i) for i in devices if i - distance in devices]
    return lax.ppermute(block, axis, route)


def activate(field):
    return jax.nn.silu(field).astype(jnp.bfloat16)


def apply_stencil(padded, flat_weight, out_rows, out_cols):
    channels = padded.shape[2]
    patches = jnp.concatenate(
        [
            padded[shift_row : shift_row + out_rows, shift_col : shift_col + out_cols]
            for shift_row in range(3)
            for shift_col in range(3)
        ],
        axis=2,
    )
    summed = jnp.dot(
        patches.reshape(out_rows * out_cols, 9 * channels),
        flat_weight,
        preferred_element_type=jnp.float32,
    )
    return summed.reshape(out_rows, out_cols, channels)


def section_pass(anchor, first_weight, second_weight, step_size):
    rows_here, cols_here, channels = anchor.shape
    widened = padded_2(anchor, (("rows", 0), ("cols", 1)), 2)
    slope_wide = apply_stencil(activate(widened), first_weight, rows_here + 2, cols_here + 2)
    middle_wide = widened[1:-1, 1:-1] + step_size * slope_wide
    row_global = lax.axis_index("rows") * rows_here - 1 + jnp.arange(rows_here + 2)
    col_global = lax.axis_index("cols") * cols_here - 1 + jnp.arange(cols_here + 2)
    inside_rows = (row_global >= 0) & (row_global < rows_here * lax.axis_size("rows"))
    inside_cols = (col_global >= 0) & (col_global < cols_here * lax.axis_size("cols"))
    inside = inside_rows[:, None] & inside_cols[None, :]
    second_act = jnp.where(inside[:, :, None], activate(middle_wide), jnp.zeros((), jnp.bfloat16))
    first_slope = slope_wide[1:-1, 1:-1]
    middle = middle_wide[1:-1, 1:-1]
    second_slope = apply_stencil(second_act, second_weight, rows_here, cols_here)
    ending = middle + step_size * second_slope
    return (first_slope, middle, ending)


def on_device(section_states, weights):
    rows_here, cols_here, channels = (
        section_states.shape[1],
        section_states.shape[2],
        section_states.shape[3],
    )
    ndepth = lax.axis_size("depth")
    position = lax.axis_index("depth")
    step_size = 2.0 / (2 * ndepth)
    first_weight = weights[0].reshape(9 * channels, channels)
    second_weight = weights[1].reshape(9 * channels, channels)
    anchor = section_states[0]
    first_slope, middle, ending = section_pass(anchor, first_weight, second_weight, step_size)
    jump = ending - (anchor + 2.0 * step_size * first_slope)

    def chain_turn(step_index, current):
        padded = padded_2(activate(current), (("rows", 0), ("cols", 1)), 1)
        advanced = (
            current
            + 2.0 * step_size * apply_stencil(padded, first_weight, rows_here, cols_here)
            + jump
        )
        shifted = shifted_2(advanced, "depth", 1)
        return jnp.where(position == 0, anchor, shifted)

    corrected = lax.fori_loop(0, ndepth - 1, chain_turn, anchor)
    final_slope, final_middle, final_ending = section_pass(
        corrected, first_weight, second_weight, step_size
    )
    fine_states = jnp.stack([final_middle, final_ending])
    return (fine_states, corrected[None])


def solution(mesh):
    in_specs = (P("depth", "rows", "cols", None), P("depth", None, None, None, None))
    out_specs = (P("depth", "rows", "cols", None), P("depth", "rows", "cols", None))
    return jax.shard_map(
        on_device, mesh=mesh, in_specs=in_specs, out_specs=out_specs, check_vma=False
    )
```

profile of v0, /device:TPU:4, one launch (start us, length us, event | category | flops | bytes accessed | tf_op | source)
XLA Modules:
  0.0 73.5 jit_solution(15360685198144042809)
XLA Ops:
  1.4 3.4 %collective-permute-start.4 = (f32[2,16,256]{2,1,0:T(8,128)S(1)}, f32[2,16,256]{2,1,0:T(8,128)S(1)}, u32[]{:S(2)}, u32[]{:S(2)}) collective-permute-start(f32[2,16,256]{2,1,0:T(8,128)S(1)} %get-tuple-element.34), channel_id=1, source_target_pairs={{0,4},{4,8},{8,12},{1,5},{5,9},{9,13},{2,6},{6,10},{10,14},{3,7},{... | collective-permute-start | bytes 98312 | tf_op jit(solution)/shard_map/ppermute | solution.py:14
  4.8 3.3 %collective-permute-start.5 = (f32[2,16,256]{2,1,0:T(8,128)S(1)}, f32[2,16,256]{2,1,0:T(8,128)S(1)}, u32[]{:S(2)}, u32[]{:S(2)}) collective-permute-start(f32[2,16,256]{2,1,0:T(8,128)S(1)} %get-tuple-element.35), channel_id=1, source_target_pairs={{4,0},{8,4},{12,8},{5,1},{9,5},{13,9},{6,2},{10,6},{14,10},{7,3},{... | collective-permute-start | bytes 98312 | tf_op jit(solution)/shard_map/ppermute | solution.py:15
  8.2 1.2 %multiply_convert_fusion.4 = bf16[32,16,256]{2,1,0:T(8,128)(2,1)S(1)} fusion(f32[1,32,16,256]{3,2,1,0:T(8,128)} %param.2), kind=kLoop, calls=%fused_computation.19 | loop fusion | flops 655360 | bytes 786432 | tf_op jit(solution)/shard_map/while/body/eval_jaxpr/convert_element_type | solution.py:27
  9.4 2.5 %collective-permute-start = (bf16[1,16,256]{2,1,0:T(8,128)(2,1)S(1)}, bf16[1,16,256]{2,1,0:T(8,128)(2,1)S(1)}, u32[]{:S(2)}, u32[]{:S(2)}) collective-permute-start(bf16[1,16,256]{2,1,0:T(8,128)(2,1)S(1)} %get-tuple-element.40), channel_id=1, source_target_pairs={{0,4},{4,8},{8,12},{1,5},{5,9},{9,13},{2,6},{6,10},{10,14},{3,7},{... | collective-permute-start | bytes 24584 | tf_op jit(solution)/shard_map/while/body/eval_jaxpr/ppermute | solution.py:14
  11.9 4.2 %collective-permute-start.1 = (bf16[1,16,256]{2,1,0:T(8,128)(2,1)S(1)}, bf16[1,16,256]{2,1,0:T(8,128)(2,1)S(1)}, u32[]{:S(2)}, u32[]{:S(2)}) collective-permute-start(bf16[1,16,256]{2,1,0:T(8,128)(2,1)S(1)} %get-tuple-element.41), channel_id=1, source_target_pairs={{4,0},{8,4},{12,8},{5,1},{9,5},{13,9},{6,2},{10,6},{14,10},{7,3},{... | collective-permute-start | bytes 24584 | tf_op jit(solution)/shard_map/while/body/eval_jaxpr/ppermute | solution.py:15
  16.1 1.8 %fusion.8 = (bf16[1,3,3,256,256]{4,3,2,1,0:T(8,128)(2,1)S(1)}, bf16[1,3,3,256,256]{4,3,2,1,0:T(8,128)(2,1)S(1)}) fusion(bf16[2,3,3,256,256]{4,3,2,1,0:T(8,128)(2,1)} %param.3), kind=kLoop, calls=%fused_computation.87 | loop fusion | bytes 4718592 | tf_op jit(solution)/shard_map/slice | solution.py:76
  18.1 3.6 %collective-permute-start.2 = (bf16[34,1,256]{2,1,0:T(2,128)(2,1)S(1)}, bf16[34,1,256]{2,1,0:T(2,128)(2,1)S(1)}, u32[]{:S(2)}, u32[]{:S(2)}) collective-permute-start(bf16[34,1,256]{2,1,0:T(2,128)(2,1)S(1)} %get-tuple-element.39), channel_id=1, source_target_pairs={{0,1},{1,2},{2,3},{4,5},{5,6},{6,7},{8,9},{9,10},{10,11},{12,13},{... | collective-permute-start | bytes 52232 | tf_op jit(solution)/shard_map/while/body/eval_jaxpr/ppermute | solution.py:14
  21.7 1.3 %collective-permute-start.3 = (bf16[34,1,256]{2,1,0:T(2,128)(2,1)S(1)}, bf16[34,1,256]{2,1,0:T(2,128)(2,1)S(1)}, u32[]{:S(2)}, u32[]{:S(2)}) collective-permute-start(bf16[34,1,256]{2,1,0:T(2,128)(2,1)S(1)} %get-tuple-element.38), channel_id=1, source_target_pairs={{1,0},{2,1},{3,2},{5,4},{6,5},{7,6},{9,8},{10,9},{11,10},{13,12},{... | collective-permute-start | bytes 52232 | tf_op jit(solution)/shard_map/while/body/eval_jaxpr/ppermute | solution.py:15
  23.3 4.2 %collective-permute-done.3 = bf16[34,1,256]{2,1,0:T(2,128)(2,1)S(1)} collective-permute-done((bf16[34,1,256]{2,1,0:T(2,128)(2,1)S(1)}, bf16[34,1,256]{2,1,0:T(2,128)(2,1)S(1)}, u32[]{:S(2)}, u32[]{:S(2)}) %collective-permute-start.3) | collective-permute-done | bytes 17440 | tf_op jit(solution)/shard_map/while/body/eval_jaxpr/ppermute | solution.py:15
  28.3 3.5 %collective-permute-start.6 = (f32[36,2,256]{2,1,0:T(2,128)S(1)}, f32[36,2,256]{2,1,0:T(2,128)S(1)}, u32[]{:S(2)}, u32[]{:S(2)}) collective-permute-start(f32[36,2,256]{2,1,0:T(2,128)S(1)} %get-tuple-element.30), channel_id=1, source_target_pairs={{0,1},{1,2},{2,3},{4,5},{5,6},{6,7},{8,9},{9,10},{10,11},{12,13},{... | collective-permute-start | bytes 221192 | tf_op jit(solution)/shard_map/ppermute | solution.py:14
  31.8 1.3 %collective-permute-start.7 = (f32[36,2,256]{2,1,0:T(2,128)S(1)}, f32[36,2,256]{2,1,0:T(2,128)S(1)}, u32[]{:S(2)}, u32[]{:S(2)}) collective-permute-start(f32[36,2,256]{2,1,0:T(2,128)S(1)} %get-tuple-element.31), channel_id=1, source_target_pairs={{1,0},{2,1},{3,2},{5,4},{6,5},{7,6},{9,8},{10,9},{11,10},{13,12},{... | collective-permute-start | bytes 221192 | tf_op jit(solution)/shard_map/ppermute | solution.py:15
  33.8 4.3 %collective-permute-done.7 = f32[36,2,256]{2,1,0:T(2,128)S(1)} collective-permute-done((f32[36,2,256]{2,1,0:T(2,128)S(1)}, f32[36,2,256]{2,1,0:T(2,128)S(1)}, u32[]{:S(2)}, u32[]{:S(2)}) %collective-permute-start.7) | collective-permute-done | bytes 73760 | tf_op jit(solution)/shard_map/ppermute | solution.py:15
  39.5 1.3 %fusion.4 = (bf16[34,18,256]{2,1,0:T(8,128)(2,1)S(1)}, f32[34,18,256]{2,1,0:T(8,128)S(1)}, f32[34,18,256]{2,1,0:T(8,128)S(1)}) fusion(pred[34,18]{1,0:T(8,128)(4,1)S(1)} %broadcast_and_fusion, f32[36,20,256]{2,1,0:T(8,128)S(1)} %get-tuple-element.26, bf16[34,18,2304]{2,1,0:T(8,128)(2,1)S(1)} %slice_dynamic-update-slice_fusion.9, ...), kind=kOutput, calls=%fused_computation.41 | convolution fusion | flops 723197952 | bytes 6193764 | tf_op jit(solution)/shard_map/dot_general | solution.py:40
  42.2 1.6 %fusion = f32[32,16,256]{2,1,0:T(8,128)} fusion(bf16[32,16,2304]{2,1,0:T(8,128)(2,1)S(1)} %slice_dynamic-update-slice_fusion.36, bf16[2304,256,1]{1,0,2:T(8,128)(2,1)S(1)} %bitcast.35, f32[34,18,256]{2,1,0:T(8,128)S(1)} %get-tuple-element.42, f32[32,16,256]{2,1,0:T(8,128)S(1)} %convolution_multiply_fusion.2, f32[34,18,256]{2,1,0:T(8,128)S(1)} %get-tuple-element.15, ...), kind=kOutput, calls=%fused_computation.4 | convolution fusion | flops 604635136 | bytes 6160384 | tf_op jit(solution)/shard_map/while/body/eval_jaxpr/dot_general | solution.py:40
  43.9 2.1 %collective-permute-start.8 = (f32[32,16,256]{2,1,0:T(8,128)}, f32[32,16,256]{2,1,0:T(8,128)}, u32[]{:S(2)}, u32[]{:S(2)}) collective-permute-start(f32[32,16,256]{2,1,0:T(8,128)} %fusion), channel_id=1, source_target_pairs={{0,16},{1,17},{2,18},{3,19},{4,20},{5,21},{6,22},{7,23},{8,24},{9,... | collective-permute-start | bytes 1572872 | tf_op jit(solution)/shard_map/while/body/eval_jaxpr/ppermute | solution.py:23
  46.0 1.1 %collective-permute-done.8 = f32[32,16,256]{2,1,0:T(8,128)} collective-permute-done((f32[32,16,256]{2,1,0:T(8,128)}, f32[32,16,256]{2,1,0:T(8,128)}, u32[]{:S(2)}, u32[]{:S(2)}) %collective-permute-start.8) | collective-permute-done | bytes 524320 | tf_op jit(solution)/shard_map/while/body/eval_jaxpr/ppermute | solution.py:23
  47.1 4.4 %collective-permute-start.10 = (f32[2,16,256]{2,1,0:T(8,128)S(1)}, f32[2,16,256]{2,1,0:T(8,128)S(1)}, u32[]{:S(2)}, u32[]{:S(2)}) collective-permute-start(f32[2,16,256]{2,1,0:T(8,128)S(1)} %get-tuple-element.33), channel_id=1, source_target_pairs={{4,0},{8,4},{12,8},{5,1},{9,5},{13,9},{6,2},{10,6},{14,10},{7,3},{... | collective-permute-start | bytes 98312 | tf_op jit(solution)/shard_map/ppermute | solution.py:15
  51.5 1.9 %collective-permute-start.9 = (f32[2,16,256]{2,1,0:T(8,128)S(1)}, f32[2,16,256]{2,1,0:T(8,128)S(1)}, u32[]{:S(2)}, u32[]{:S(2)}) collective-permute-start(f32[2,16,256]{2,1,0:T(8,128)S(1)} %get-tuple-element.32), channel_id=1, source_target_pairs={{0,4},{4,8},{8,12},{1,5},{5,9},{9,13},{2,6},{6,10},{10,14},{3,7},{... | collective-permute-start | bytes 98312 | tf_op jit(solution)/shard_map/ppermute | solution.py:14
  53.5 5.0 %collective-permute-done.9 = f32[2,16,256]{2,1,0:T(8,128)S(1)} collective-permute-done((f32[2,16,256]{2,1,0:T(8,128)S(1)}, f32[2,16,256]{2,1,0:T(8,128)S(1)}, u32[]{:S(2)}, u32[]{:S(2)}) %collective-permute-start.9) | collective-permute-done | bytes 32800 | tf_op jit(solution)/shard_map/ppermute | solution.py:14
  58.5 3.5 %collective-permute-start.11 = (f32[36,2,256]{2,1,0:T(2,128)S(1)}, f32[36,2,256]{2,1,0:T(2,128)S(1)}, u32[]{:S(2)}, u32[]{:S(2)}) collective-permute-start(f32[36,2,256]{2,1,0:T(2,128)S(1)} %get-tuple-element.28), channel_id=1, source_target_pairs={{0,1},{1,2},{2,3},{4,5},{5,6},{6,7},{8,9},{9,10},{10,11},{12,13},{... | collective-permute-start | bytes 221192 | tf_op jit(solution)/shard_map/ppermute | solution.py:14
  62.0 1.3 %collective-permute-start.12 = (f32[36,2,256]{2,1,0:T(2,128)S(1)}, f32[36,2,256]{2,1,0:T(2,128)S(1)}, u32[]{:S(2)}, u32[]{:S(2)}) collective-permute-start(f32[36,2,256]{2,1,0:T(2,128)S(1)} %get-tuple-element.29), channel_id=1, source_target_pairs={{1,0},{2,1},{3,2},{5,4},{6,5},{7,6},{9,8},{10,9},{11,10},{13,12},{... | collective-permute-start | bytes 221192 | tf_op jit(solution)/shard_map/ppermute | solution.py:15
  63.9 4.3 %collective-permute-done.12 = f32[36,2,256]{2,1,0:T(2,128)S(1)} collective-permute-done((f32[36,2,256]{2,1,0:T(2,128)S(1)}, f32[36,2,256]{2,1,0:T(2,128)S(1)}, u32[]{:S(2)}, u32[]{:S(2)}) %collective-permute-start.12) | collective-permute-done | bytes 73760 | tf_op jit(solution)/shard_map/ppermute | solution.py:15
  69.7 1.4 %fusion.5 = (bf16[34,18,256]{2,1,0:T(8,128)(2,1)S(1)}, f32[34,18,256]{2,1,0:T(8,128)S(1)}) fusion(pred[34,18]{1,0:T(8,128)(4,1)S(1)} %broadcast_and_fusion, bf16[34,18,2304]{2,1,0:T(8,128)(2,1)S(1)} %slice_dynamic-update-slice_fusion, bf16[2304,256,1]{1,0,2:T(8,128)(2,1)S(1)} %bitcast.36, f32[36,20,256]{2,1,0:T(8,128)S(1)} %get-tuple-element.25), kind=kOutput, calls=%fused_computation.42 | convolution fusion | flops 723197952 | bytes 5567076 | tf_op jit(solution)/shard_map/dot_general | solution.py:40
  72.5 1.0 %pad_maximum_fusion = f32[2,32,16,256]{3,2,1,0:T(8,128)} fusion(f32[1,32,16,256]{3,2,1,0:T(8,128)S(1)} %fusion.2, f32[1,32,16,256]{3,2,1,0:T(8,128)S(1)} %slice_bitcast_fusion), kind=kLoop, calls=%fused_computation.7 | loop fusion | flops 262144 | bytes 2097152 | tf_op jit(solution)/shard_map/stack | solution.py:95
  (73 shorter events, 8.8 us)
Async XLA Ops:
  1.4 26.8 %collective-permute-start.4 = (f32[2,16,256]{2,1,0:T(8,128)S(1)}, f32[2,16,256]{2,1,0:T(8,128)S(1)}, u32[]{:S(2)}, u32[]{:S(2)}) collective-permute-start(f32[2,16,256]{2,1,0:T(8,128)S(1)} %get-tuple-element.34), channel_id=1, source_target_pairs={{0,4},{4,8},{8,12},{1,5},{5,9},{9,13},{2,6},{6,10},{10,14},{3,7},{... | collective-permute-start | bytes 98312 | tf_op jit(solution)/shard_map/ppermute | solution.py:14
  4.8 23.5 %collective-permute-start.5 = (f32[2,16,256]{2,1,0:T(8,128)S(1)}, f32[2,16,256]{2,1,0:T(8,128)S(1)}, u32[]{:S(2)}, u32[]{:S(2)}) collective-permute-start(f32[2,16,256]{2,1,0:T(8,128)S(1)} %get-tuple-element.35), channel_id=1, source_target_pairs={{4,0},{8,4},{12,8},{5,1},{9,5},{13,9},{6,2},{10,6},{14,10},{7,3},{... | collective-permute-start | bytes 98312 | tf_op jit(solution)/shard_map/ppermute | solution.py:15
  9.4 8.6 %collective-permute-start = (bf16[1,16,256]{2,1,0:T(8,128)(2,1)S(1)}, bf16[1,16,256]{2,1,0:T(8,128)(2,1)S(1)}, u32[]{:S(2)}, u32[]{:S(2)}) collective-permute-start(bf16[1,16,256]{2,1,0:T(8,128)(2,1)S(1)} %get-tuple-element.40), channel_id=1, source_target_pairs={{0,4},{4,8},{8,12},{1,5},{5,9},{9,13},{2,6},{6,10},{10,14},{3,7},{... | collective-permute-start | bytes 24584 | tf_op jit(solution)/shard_map/while/body/eval_jaxpr/ppermute | solution.py:14
  11.9 6.1 %collective-permute-start.1 = (bf16[1,16,256]{2,1,0:T(8,128)(2,1)S(1)}, bf16[1,16,256]{2,1,0:T(8,128)(2,1)S(1)}, u32[]{:S(2)}, u32[]{:S(2)}) collective-permute-start(bf16[1,16,256]{2,1,0:T(8,128)(2,1)S(1)} %get-tuple-element.41), channel_id=1, source_target_pairs={{4,0},{8,4},{12,8},{5,1},{9,5},{13,9},{6,2},{10,6},{14,10},{7,3},{... | collective-permute-start | bytes 24584 | tf_op jit(solution)/shard_map/while/body/eval_jaxpr/ppermute | solution.py:15
  18.0 10.0 %copy-start = (f32[1,32,16,256]{3,2,1,0:T(8,128)S(1)}, f32[1,32,16,256]{3,2,1,0:T(8,128)}, u32[]{:S(2)}) copy-start(f32[1,32,16,256]{3,2,1,0:T(8,128)} %param.2) | copy-start | bytes 1572868
  18.1 5.2 %collective-permute-start.2 = (bf16[34,1,256]{2,1,0:T(2,128)(2,1)S(1)}, bf16[34,1,256]{2,1,0:T(2,128)(2,1)S(1)}, u32[]{:S(2)}, u32[]{:S(2)}) collective-permute-start(bf16[34,1,256]{2,1,0:T(2,128)(2,1)S(1)} %get-tuple-element.39), channel_id=1, source_target_pairs={{0,1},{1,2},{2,3},{4,5},{5,6},{6,7},{8,9},{9,10},{10,11},{12,13},{... | collective-permute-start | bytes 52232 | tf_op jit(solution)/shard_map/while/body/eval_jaxpr/ppermute | solution.py:14
  21.7 5.8 %collective-permute-start.3 = (bf16[34,1,256]{2,1,0:T(2,128)(2,1)S(1)}, bf16[34,1,256]{2,1,0:T(2,128)(2,1)S(1)}, u32[]{:S(2)}, u32[]{:S(2)}) collective-permute-start(bf16[34,1,256]{2,1,0:T(2,128)(2,1)S(1)} %get-tuple-element.38), channel_id=1, source_target_pairs={{1,0},{2,1},{3,2},{5,4},{6,5},{7,6},{9,8},{10,9},{11,10},{13,12},{... | collective-permute-start | bytes 52232 | tf_op jit(solution)/shard_map/while/body/eval_jaxpr/ppermute | solution.py:15
  28.3 5.5 %collective-permute-start.6 = (f32[36,2,256]{2,1,0:T(2,128)S(1)}, f32[36,2,256]{2,1,0:T(2,128)S(1)}, u32[]{:S(2)}, u32[]{:S(2)}) collective-permute-start(f32[36,2,256]{2,1,0:T(2,128)S(1)} %get-tuple-element.30), channel_id=1, source_target_pairs={{0,1},{1,2},{2,3},{4,5},{5,6},{6,7},{8,9},{9,10},{10,11},{12,13},{... | collective-permute-start | bytes 221192 | tf_op jit(solution)/shard_map/ppermute | solution.py:14
  31.8 6.2 %collective-permute-start.7 = (f32[36,2,256]{2,1,0:T(2,128)S(1)}, f32[36,2,256]{2,1,0:T(2,128)S(1)}, u32[]{:S(2)}, u32[]{:S(2)}) collective-permute-start(f32[36,2,256]{2,1,0:T(2,128)S(1)} %get-tuple-element.31), channel_id=1, source_target_pairs={{1,0},{2,1},{3,2},{5,4},{6,5},{7,6},{9,8},{10,9},{11,10},{13,12},{... | collective-permute-start | bytes 221192 | tf_op jit(solution)/shard_map/ppermute | solution.py:15
  43.9 3.1 %collective-permute-start.8 = (f32[32,16,256]{2,1,0:T(8,128)}, f32[32,16,256]{2,1,0:T(8,128)}, u32[]{:S(2)}, u32[]{:S(2)}) collective-permute-start(f32[32,16,256]{2,1,0:T(8,128)} %fusion), channel_id=1, source_target_pairs={{0,16},{1,17},{2,18},{3,19},{4,20},{5,21},{6,22},{7,23},{8,24},{9,... | collective-permute-start | bytes 1572872 | tf_op jit(solution)/shard_map/while/body/eval_jaxpr/ppermute | solution.py:23
  47.1 21.8 %copy-start.1 = (f32[32,16,256]{2,1,0:T(8,128)}, f32[32,16,256]{2,1,0:T(8,128)S(1)}, u32[]{:S(2)}) copy-start(f32[32,16,256]{2,1,0:T(8,128)S(1)} %broadcast_select_fusion) | copy-start | bytes 1572868
  47.1 6.3 %collective-permute-start.10 = (f32[2,16,256]{2,1,0:T(8,128)S(1)}, f32[2,16,256]{2,1,0:T(8,128)S(1)}, u32[]{:S(2)}, u32[]{:S(2)}) collective-permute-start(f32[2,16,256]{2,1,0:T(8,128)S(1)} %get-tuple-element.33), channel_id=1, source_target_pairs={{4,0},{8,4},{12,8},{5,1},{9,5},{13,9},{6,2},{10,6},{14,10},{7,3},{... | collective-permute-start | bytes 98312 | tf_op jit(solution)/shard_map/ppermute | solution.py:15
  51.5 6.9 %collective-permute-start.9 = (f32[2,16,256]{2,1,0:T(8,128)S(1)}, f32[2,16,256]{2,1,0:T(8,128)S(1)}, u32[]{:S(2)}, u32[]{:S(2)}) collective-permute-start(f32[2,16,256]{2,1,0:T(8,128)S(1)} %get-tuple-element.32), channel_id=1, source_target_pairs={{0,4},{4,8},{8,12},{1,5},{5,9},{9,13},{2,6},{6,10},{10,14},{3,7},{... | collective-permute-start | bytes 98312 | tf_op jit(solution)/shard_map/ppermute | solution.py:14
  58.5 5.5 %collective-permute-start.11 = (f32[36,2,256]{2,1,0:T(2,128)S(1)}, f32[36,2,256]{2,1,0:T(2,128)S(1)}, u32[]{:S(2)}, u32[]{:S(2)}) collective-permute-start(f32[36,2,256]{2,1,0:T(2,128)S(1)} %get-tuple-element.28), channel_id=1, source_target_pairs={{0,1},{1,2},{2,3},{4,5},{5,6},{6,7},{8,9},{9,10},{10,11},{12,13},{... | collective-permute-start | bytes 221192 | tf_op jit(solution)/shard_map/ppermute | solution.py:14
  62.0 6.2 %collective-permute-start.12 = (f32[36,2,256]{2,1,0:T(2,128)S(1)}, f32[36,2,256]{2,1,0:T(2,128)S(1)}, u32[]{:S(2)}, u32[]{:S(2)}) collective-permute-start(f32[36,2,256]{2,1,0:T(2,128)S(1)} %get-tuple-element.29), channel_id=1, source_target_pairs={{1,0},{2,1},{3,2},{5,4},{6,5},{7,6},{9,8},{10,9},{11,10},{13,12},{... | collective-permute-start | bytes 221192 | tf_op jit(solution)/shard_map/ppermute | solution.py:15
where the time goes:
time: 74.2 us; the launch traced here: 73.5 us
  starting transfers between devices  36.3 us (49%)
  waiting for transfers between devices  20.3 us (27%)
  local copies, waits for them, and re-layouts  6.26 us (8%)
  matrix products  5.88 us (8%)
  other arithmetic  3.59 us (5%)
  between operations  1.19 us (2%)
    ppermute x6, starting transfers between devices, padded_2(): before = lax.ppermute(last, axis, up)  18.4 us
    ppermute x6, starting transfers between devices, padded_2(): after = lax.ppermute(initial, axis, down)  15.9 us
    ppermute x6, waiting for transfers between devices, padded_2(): after = lax.ppermute(initial, axis, down)  12.8 us
    ppermute x6, waiting for transfers between devices, padded_2(): before = lax.ppermute(last, axis, up)  6.41 us
    dot_general x5, matrix products, apply_stencil(): jnp.dot(patches.reshape(out_rows * out_cols, 9 * channels), flat_weight,...  5.88 us
    unnamed x41, local copies, waits for them, and re-layouts  3.02 us
    ppermute x1, starting transfers between devices, shifted_2(): return lax.ppermute(block, axis, route)  2.09 us
    slice x1, local copies, waits for them, and re-layouts, on_device(): second_weight = weights[1].reshape(9 * channels, channels)  1.81 us
  transfers between devices with their start and end apart: 13, of which 8 were waited for; matrix products, arithmetic and copies ran while one was open for 5% of the time, Pallas kernels for 0%

commit v1 on v0

--- a/solution.py
+++ b/solution.py
@@ -1,7 +1,15 @@
+import functools
+
 import jax
 import jax.numpy as jnp
 from jax import lax
+from jax.experimental import pallas as pl
+from jax.experimental.pallas import tpu as pltpu
 from jax.sharding import PartitionSpec as P
+
+MESH = pl.DeviceIdType.MESH
+HALO = 4
+LANES = 128
 
 
 def padded_2(shard, sides, width):
@@ -63,12 +71,8 @@
     return (first_slope, middle, ending)
 
 
-def on_device(section_states, weights):
-    rows_here, cols_here, channels = (
-        section_states.shape[1],
-        section_states.shape[2],
-        section_states.shape[3],
-    )
+def chain_on_device(section_states, weights):
+    rows_here, cols_here, channels = section_states.shape[1:]
     ndepth = lax.axis_size("depth")
     position = lax.axis_index("depth")
     step_size = 2.0 / (2 * ndepth)
@@ -96,6 +100,333 @@
     return (fine_states, corrected[None])
 
 
+def largest_divisor(total, limit):
+    return max(n for n in range(1, limit + 1) if total % n == 0)
+
+
+DIRECTIONS = ((-1, 0), (1, 0), (0, -1), (0, 1), (-1, -1), (-1, 1), (1, -1), (1, 1))
+
+
+def cycle_kernel(
+    sizes, x_hbm, w_hbm, fine_hbm, coarse_hbm,
+    x, w, base, mid, end, act0, act1, patches, stage,
+    flat, send_row, send_col, recv_row, recv_col, recv_corner,
+    load_sem, store_sem, send_sem, recv_sem, pass_send, pass_recv,
+):
+    nrows, ncols, step_size = sizes
+    rows_here, cols_here, channels = x.shape
+    halves = channels // LANES
+    high, wide = rows_here + 2 * HALO, cols_here + 2 * HALO
+    depth, row, col = lax.axis_index("depth"), lax.axis_index("rows"), lax.axis_index("cols")
+
+    x_load = pltpu.make_async_copy(x_hbm.at[0], x, load_sem.at[0])
+    w_loads = [pltpu.make_async_copy(w_hbm.at[k], w.at[k], load_sem.at[1 + k]) for k in range(2)]
+
+    barrier = pltpu.get_barrier_semaphore()
+
+    def neighbour(step):
+        there_row, there_col = row + step[0], col + step[1]
+        exists = (there_row >= 0) & (there_row < nrows) & (there_col >= 0) & (there_col < ncols)
+        return exists, (depth, there_row, there_col)
+
+    @pl.when(depth == 0)
+    def _():
+        x_load.start()
+
+    for copy in w_loads:
+        copy.start()
+    pl.semaphore_signal(barrier, inc=1, device_id=(1 - depth, row, col), device_id_type=MESH)
+
+    @pl.when(depth == 0)
+    def _():
+        for step in DIRECTIONS:
+            exists, target = neighbour(step)
+
+            @pl.when(exists)
+            def _():
+                pl.semaphore_signal(barrier, inc=1, device_id=target, device_id_type=MESH)
+
+    def halves_of(c):
+        return pl.ds(c * LANES, LANES)
+
+    def masked_silu(u, first_row):
+        n = u.shape[0]
+        i = first_row + lax.broadcasted_iota(jnp.int32, (n, wide, LANES), 0) + (row * rows_here - HALO)
+        j = lax.broadcasted_iota(jnp.int32, (n, wide, LANES), 1) + (col * cols_here - HALO)
+        inside = (i >= 0) & (i < nrows * rows_here) & (j >= 0) & (j < ncols * cols_here)
+        return jnp.where(inside, u / (1.0 + jnp.exp(-u)), 0.0)
+
+    def slopes(act, layer, first_row, n, left, width):
+        m = n * width
+        for a in range(3):
+            for b in range(3):
+                for c in range(halves):
+                    window = act[c, pl.ds(first_row + a - 1, n), left + b : left + b + width, :]
+                    patches[0:m, pl.ds((a * 3 + b) * channels + c * LANES, LANES)] = (
+                        window.reshape(m, LANES).astype(jnp.bfloat16)
+                    )
+        acc = jnp.dot(patches[0:m, :], w[layer], preferred_element_type=jnp.float32)
+        return [
+            step_size * acc[:, c * LANES : (c + 1) * LANES].reshape(n, width, LANES)
+            for c in range(halves)
+        ]
+
+    def stage_interior(state, slot):
+        def body(i, _):
+            for c in range(halves):
+                stage[slot, i, :, halves_of(c)] = state[c, i + HALO, HALO : HALO + cols_here, :]
+            return 0
+
+        lax.fori_loop(0, rows_here, body, 0, unroll=4)
+
+    def store(slot, ref):
+        return pltpu.make_async_copy(stage.at[slot], ref, store_sem.at[slot])
+
+    end_rows = high - 4
+    piece = largest_divisor(end_rows, 12)
+    pieces = end_rows // piece
+
+    def hand_over(k):
+        rows = pl.ds(2 + k * piece, piece)
+        return pltpu.make_async_remote_copy(
+            src_ref=end.at[:, rows], dst_ref=end.at[:, rows],
+            send_sem=pass_send.at[k], recv_sem=pass_recv.at[k],
+            device_id=(1 - depth, row, col), device_id_type=MESH,
+        )
+
+    def first_layer(source, target, first_row, total, limit):
+        n = largest_divisor(total, limit)
+
+        def body(k, _):
+            at = first_row + k * n
+            rise = slopes(act0, 0, at, n, 0, wide)
+            for c in range(halves):
+                u = source[c, pl.ds(at, n)] + rise[c]
+                target[c, pl.ds(at, n)] = u
+                act1[c, pl.ds(at, n), 1 : 1 + wide, :] = masked_silu(u, at)
+            return 0
+
+        lax.fori_loop(0, total // n, body, 0)
+
+    @pl.when(depth == 0)
+    def _():
+        x_load.wait()
+        coarse_store = pltpu.make_async_copy(x, coarse_hbm.at[0], store_sem.at[2])
+        coarse_store.start()
+        for side in range(2):
+            rows_from = 0 if side == 0 else rows_here - HALO
+            cols_from = 0 if side == 0 else cols_here - HALO
+            send_row[side] = (
+                x[rows_from : rows_from + HALO].reshape(HALO * cols_here, channels).astype(jnp.bfloat16)
+            )
+            for i in range(rows_here):
+                for c in range(halves):
+                    flat[side, c, i * HALO : (i + 1) * HALO, :] = x[
+                        i, cols_from : cols_from + HALO, c * LANES : (c + 1) * LANES
+                    ]
+            for c in range(halves):
+                send_col[side, :, halves_of(c)] = flat[side, c].astype(jnp.bfloat16)
+        peers = jnp.int32(1)
+        for step in DIRECTIONS:
+            exists, target = neighbour(step)
+            peers = peers + jnp.where(exists, 1, 0)
+        pl.semaphore_wait(barrier, peers)
+
+        corner = HALO * HALO
+        copies = []
+        for k, (dr, dc) in enumerate(DIRECTIONS):
+            exists, target = neighbour((dr, dc))
+            if dc == 0:
+                side = (dr + 1) // 2
+                src, dst = send_row.at[side], recv_row.at[1 - side]
+            elif dr == 0:
+                side = (dc + 1) // 2
+                src, dst = send_col.at[side], recv_col.at[1 - side]
+            else:
+                side = (dc + 1) // 2
+                from_row = 0 if dr < 0 else (rows_here - HALO) * HALO
+                src = send_col.at[side, pl.ds(from_row, corner)]
+                dst = recv_corner.at[(1 - dr) // 2, (1 - dc) // 2]
+            opposite = DIRECTIONS.index((-dr, -dc))
+            copy = pltpu.make_async_remote_copy(
+                src_ref=src, dst_ref=dst, send_sem=send_sem.at[k], recv_sem=recv_sem.at[opposite],
+                device_id=target, device_id_type=MESH,
+            )
+            arrival = pltpu.make_async_remote_copy(
+                src_ref=src,
+                dst_ref=(
+                    recv_row.at[(dr + 1) // 2] if dc == 0
+                    else recv_col.at[(dc + 1) // 2] if dr == 0
+                    else recv_corner.at[(dr + 1) // 2, (dc + 1) // 2]
+                ),
+                send_sem=send_sem.at[k], recv_sem=recv_sem.at[k],
+                device_id=target, device_id_type=MESH,
+            )
+            copies.append((exists, copy, arrival))
+        order = (4, 5, 6, 7, 2, 3, 0, 1)
+        for k in order:
+            exists, copy, arrival = copies[k]
+            pl.when(exists)(copy.start)
+
+        def place(i, _):
+            for c in range(halves):
+                base[c, i + HALO, HALO : HALO + cols_here, :] = x[i, :, halves_of(c)]
+            return 0
+
+        lax.fori_loop(0, rows_here, place, 0, unroll=4)
+
+        for exists, copy, arrival in copies:
+
+            @pl.when(exists)
+            def _(copy=copy, arrival=arrival):
+                arrival.wait_recv()
+
+        for side in range(2):
+            top = 0 if side == 0 else high - HALO
+            left = 0 if side == 0 else wide - HALO
+            for c in range(halves):
+                base[c, top : top + HALO, HALO : HALO + cols_here, :] = (
+                    recv_row[side, :, halves_of(c)].astype(jnp.float32).reshape(HALO, cols_here, LANES)
+                )
+                flat[side, c] = recv_col[side, :, halves_of(c)].astype(jnp.float32)
+                for i in range(rows_here):
+                    base[c, HALO + i, left : left + HALO, :] = flat[side, c, i * HALO : (i + 1) * HALO, :]
+            for other in range(2):
+                beside = 0 if other == 0 else wide - HALO
+                for c in range(halves):
+                    block = recv_corner[side, other, :, halves_of(c)].astype(jnp.float32)
+                    for i in range(HALO):
+                        base[c, top + i, beside : beside + HALO, :] = block[i * HALO : (i + 1) * HALO]
+
+        n = largest_divisor(high, 8)
+
+        def start_act(k, _):
+            for c in range(halves):
+                u = base[c, pl.ds(k * n, n)]
+                act0[c, pl.ds(k * n, n), 1 : 1 + wide, :] = masked_silu(u, k * n)
+            return 0
+
+        lax.fori_loop(0, high // n, start_act, 0)
+        w_loads[0].wait()
+        first_layer(base, mid, 1, high - 2, 19)
+        stage_interior(mid, 0)
+        store(0, fine_hbm.at[0]).start()
+        w_loads[1].wait()
+
+        def second(k, _):
+            at = 2 + k * piece
+            rise = slopes(act1, 1, at, piece, 0, wide)
+            for c in range(halves):
+                end[c, pl.ds(at, piece)] = mid[c, pl.ds(at, piece)] + rise[c]
+            hand_over(k).start()
+            return 0
+
+        lax.fori_loop(0, pieces, second, 0)
+        stage_interior(end, 1)
+        store(1, fine_hbm.at[1]).start()
+        for exists, copy, arrival in copies:
+
+            @pl.when(exists)
+            def _(copy=copy):
+                copy.wait_send()
+
+        def sent(k, _):
+            hand_over(k).wait_send()
+            return 0
+
+        lax.fori_loop(0, pieces, sent, 0)
+        coarse_store.wait()
+        store(0, fine_hbm.at[0]).wait()
+        store(1, fine_hbm.at[1]).wait()
+
+    @pl.when(depth == 1)
+    def _():
+        pl.semaphore_wait(barrier, 1)
+
+        def received(k, _):
+            hand_over(k).wait_recv()
+            at = 2 + k * piece
+            for c in range(halves):
+                u = end[c, pl.ds(at, piece)]
+                act0[c, pl.ds(at, piece), 1 : 1 + wide, :] = masked_silu(u, at)
+            return 0
+
+        lax.fori_loop(0, pieces, received, 0)
+        stage_interior(end, 2)
+        store(2, coarse_hbm.at[0]).start()
+        w_loads[0].wait()
+        first_layer(end, mid, 3, high - 6, 17)
+        stage_interior(mid, 0)
+        store(0, fine_hbm.at[0]).start()
+        w_loads[1].wait()
+        n = largest_divisor(rows_here, 16)
+
+        def last(k, _):
+            at = k * n
+            rise = slopes(act1, 1, at + HALO, n, HALO, cols_here)
+            for c in range(halves):
+                stage[1, pl.ds(at, n), :, halves_of(c)] = stage[0, pl.ds(at, n), :, halves_of(c)] + rise[c]
+            return 0
+
+        lax.fori_loop(0, rows_here // n, last, 0)
+        store(1, fine_hbm.at[1]).start()
+        store(2, coarse_hbm.at[0]).wait()
+        store(0, fine_hbm.at[0]).wait()
+        store(1, fine_hbm.at[1]).wait()
+
+
+def two_sections(section_states, weights):
+    _, rows_here, cols_here, channels = section_states.shape
+    halves = channels // LANES
+    high, wide = rows_here + 2 * HALO, cols_here + 2 * HALO
+    act_wide = -(-(wide + 2) // 8) * 8
+    pieces = (high - 4) // largest_divisor(high - 4, 12)
+    sizes = (lax.axis_size("rows"), lax.axis_size("cols"), 2.0 / (2 * lax.axis_size("depth")))
+    f32, bf16, vmem = jnp.float32, jnp.bfloat16, pltpu.VMEM
+    state = vmem((halves, high, wide, LANES), f32)
+    act = vmem((halves, high, act_wide, LANES), f32)
+    most = max(largest_divisor(high - 2, 19), largest_divisor(high - 6, 17), largest_divisor(high - 4, 12))
+    most_pixels = max(most * wide, largest_divisor(rows_here, 16) * cols_here)
+    flat_weights = weights.reshape(2, 9 * channels, channels)
+    return pl.pallas_call(
+        functools.partial(cycle_kernel, sizes),
+        out_shape=(
+            jax.ShapeDtypeStruct((2, rows_here, cols_here, channels), f32),
+            jax.ShapeDtypeStruct((1, rows_here, cols_here, channels), f32),
+        ),
+        in_specs=[pl.BlockSpec(memory_space=pl.ANY)] * 2,
+        out_specs=[pl.BlockSpec(memory_space=pl.ANY)] * 2,
+        scratch_shapes=[
+            vmem((rows_here, cols_here, channels), f32),
+            vmem((2, 9 * channels, channels), bf16),
+            state, state, state, act, act,
+            vmem((-(-most_pixels // 16) * 16, 9 * channels), bf16),
+            vmem((3, rows_here, cols_here, channels), f32),
+            vmem((2, halves, rows_here * HALO, LANES), f32),
+            vmem((2, HALO * cols_here, channels), bf16),
+            vmem((2, rows_here * HALO, channels), bf16),
+            vmem((2, HALO * cols_here, channels), bf16),
+            vmem((2, rows_here * HALO, channels), bf16),
+            vmem((2, 2, HALO * HALO, channels), bf16),
+            pltpu.SemaphoreType.DMA((3,)),
+            pltpu.SemaphoreType.DMA((3,)),
+            pltpu.SemaphoreType.DMA((8,)),
+            pltpu.SemaphoreType.DMA((8,)),
+            pltpu.SemaphoreType.DMA((pieces,)),
+            pltpu.SemaphoreType.DMA((pieces,)),
+        ],
+        compiler_params=pltpu.CompilerParams(collective_id=0, has_side_effects=True),
+    )(section_states, flat_weights)
+
+
+def on_device(section_states, weights):
+    _, rows_here, cols_here, channels = section_states.shape
+    tiles = rows_here % 8 == 0 and cols_here % 8 == 0 and channels % LANES == 0
+    if lax.axis_size("depth") == 2 and tiles and min(rows_here, cols_here) >= HALO:
+        return two_sections(section_states, weights)
+    return chain_on_device(section_states, weights)
+
+
 def solution(mesh):
     in_specs = (P("depth", "rows", "cols", None), P("depth", None, None, None, None))
     out_specs = (P("depth", "rows", "cols", None), P("depth", "rows", "cols", None))

time: 74.2 us -> 20.9 us (0.28)
  the two profiles are of different devices: /device:TPU:4 before, /device:TPU:1 now
where the time goes in v1:
time: 20.9 us; the launch traced here: 20.8 us
  Pallas kernels  17 us (81%)
  local copies, waits for them, and re-layouts  3.12 us (15%)
  between operations  0.65 us (3%)
    pallas_call x1, Pallas kernels, two_sections(): pl.pallas_call(functools.partial(cycle_kernel, sizes), out_shape=(jax.Sha...  17 us
    unnamed x4, local copies, waits for them, and re-layouts  3.12 us

profile of v1, /device:TPU:1, one launch (start us, length us, event | category | flops | bytes accessed | tf_op | source)
XLA Modules:
  0.0 20.8 jit_solution(2141079655090196434)
XLA Ops:
  0.6 17.0 %shard_map.41 = (f32[2,32,16,256]{3,2,1,0:T(8,128)}, f32[1,32,16,256]{3,2,1,0:T(8,128)}) custom-call(f32[1,32,16,256]{3,2,1,0:T(8,128)} %x_hbm.1, bf16[2,2304,256]{2,1,0:T(8,128)(2,1)} %bitcast.1), custom_call_target="tpu_custom_call" | custom-call | tf_op jit(solution)/shard_map/pallas_call | solution.py:391
  17.6 0.0 copy-start
  17.6 2.3 %copy.6 = f32[2,32,16,256]{3,2,1,0:T(8,128)} copy(f32[2,32,16,256]{3,2,1,0:T(8,128)} %get-tuple-element.4) | data formatting | bytes 2097152
  20.0 0.0 copy-done
  20.0 0.8 %copy.7 = f32[1,32,16,256]{3,2,1,0:T(8,128)} copy(f32[1,32,16,256]{3,2,1,0:T(8,128)S(1)} %copy-done) | data formatting | bytes 1048576
Async XLA Ops:
  17.6 2.3 %copy-start = (f32[1,32,16,256]{3,2,1,0:T(8,128)S(1)}, f32[1,32,16,256]{3,2,1,0:T(8,128)}, u32[]{:S(2)}) copy-start(f32[1,32,16,256]{3,2,1,0:T(8,128)} %get-tuple-element.5) | copy-start | bytes 1572868

commit v2 on v1

--- a/solution.py
+++ b/solution.py
@@ -10,6 +10,7 @@
 MESH = pl.DeviceIdType.MESH
 HALO = 4
 LANES = 128
+LIMIT = 32 * 1024 * 1024
 
 
 def padded_2(shard, sides, width):
@@ -108,19 +109,21 @@
 
 
 def cycle_kernel(
-    sizes, x_hbm, w_hbm, fine_hbm, coarse_hbm,
-    x, w, base, mid, end, act0, act1, patches, stage,
+    sizes, x_hbm, w_hbm, act1, w_last, stage,
+    w_first, base, mid, end, act0, patches,
     flat, send_row, send_col, recv_row, recv_col, recv_corner,
-    load_sem, store_sem, send_sem, recv_sem, pass_send, pass_recv,
+    load_sem, send_sem, recv_sem, pass_send, pass_recv,
 ):
     nrows, ncols, step_size = sizes
+    x = stage.at[2]
+    w = (w_first, w_last)
     rows_here, cols_here, channels = x.shape
     halves = channels // LANES
     high, wide = rows_here + 2 * HALO, cols_here + 2 * HALO
     depth, row, col = lax.axis_index("depth"), lax.axis_index("rows"), lax.axis_index("cols")
 
     x_load = pltpu.make_async_copy(x_hbm.at[0], x, load_sem.at[0])
-    w_loads = [pltpu.make_async_copy(w_hbm.at[k], w.at[k], load_sem.at[1 + k]) for k in range(2)]
+    w_loads = [pltpu.make_async_copy(w_hbm.at[k], w[k], load_sem.at[1 + k]) for k in range(2)]
 
     barrier = pltpu.get_barrier_semaphore()
 
@@ -165,7 +168,7 @@
                     patches[0:m, pl.ds((a * 3 + b) * channels + c * LANES, LANES)] = (
                         window.reshape(m, LANES).astype(jnp.bfloat16)
                     )
-        acc = jnp.dot(patches[0:m, :], w[layer], preferred_element_type=jnp.float32)
+        acc = jnp.dot(patches[0:m, :], w[layer][...], preferred_element_type=jnp.float32)
         return [
             step_size * acc[:, c * LANES : (c + 1) * LANES].reshape(n, width, LANES)
             for c in range(halves)
@@ -178,9 +181,6 @@
             return 0
 
         lax.fori_loop(0, rows_here, body, 0, unroll=4)
-
-    def store(slot, ref):
-        return pltpu.make_async_copy(stage.at[slot], ref, store_sem.at[slot])
 
     end_rows = high - 4
     piece = largest_divisor(end_rows, 12)
@@ -211,8 +211,6 @@
     @pl.when(depth == 0)
     def _():
         x_load.wait()
-        coarse_store = pltpu.make_async_copy(x, coarse_hbm.at[0], store_sem.at[2])
-        coarse_store.start()
         for side in range(2):
             rows_from = 0 if side == 0 else rows_here - HALO
             cols_from = 0 if side == 0 else cols_here - HALO
@@ -310,7 +308,6 @@
         w_loads[0].wait()
         first_layer(base, mid, 1, high - 2, 19)
         stage_interior(mid, 0)
-        store(0, fine_hbm.at[0]).start()
         w_loads[1].wait()
 
         def second(k, _):
@@ -323,7 +320,6 @@
 
         lax.fori_loop(0, pieces, second, 0)
         stage_interior(end, 1)
-        store(1, fine_hbm.at[1]).start()
         for exists, copy, arrival in copies:
 
             @pl.when(exists)
@@ -335,9 +331,6 @@
             return 0
 
         lax.fori_loop(0, pieces, sent, 0)
-        coarse_store.wait()
-        store(0, fine_hbm.at[0]).wait()
-        store(1, fine_hbm.at[1]).wait()
 
     @pl.when(depth == 1)
     def _():
@@ -353,26 +346,62 @@
 
         lax.fori_loop(0, pieces, received, 0)
         stage_interior(end, 2)
-        store(2, coarse_hbm.at[0]).start()
         w_loads[0].wait()
         first_layer(end, mid, 3, high - 6, 17)
         stage_interior(mid, 0)
-        store(0, fine_hbm.at[0]).start()
         w_loads[1].wait()
-        n = largest_divisor(rows_here, 16)
+
+
+def last_kernel(
+    step_size, act, w, stage, fine_hbm, coarse_hbm, patches, ending, store_sem, piece_sem
+):
+    _, rows_here, cols_here, channels = stage.shape
+    halves = channels // LANES
+    depth = lax.axis_index("depth")
+    pieces = piece_sem.shape[0]
+    n = rows_here // pieces
+    m = n * cols_here
+
+    def store(slot, ref):
+        return pltpu.make_async_copy(stage.at[slot], ref, store_sem.at[slot])
+
+    coarse_store = store(2, coarse_hbm.at[0])
+    first_store = store(0, fine_hbm.at[0])
+    coarse_store.start()
+    first_store.start()
+
+    @pl.when(depth == 0)
+    def _():
+        second_store = store(1, fine_hbm.at[1])
+        second_store.start()
+        second_store.wait()
+
+    @pl.when(depth == 1)
+    def _():
+        def piece_store(k):
+            rows = pl.ds(k * n, n)
+            return pltpu.make_async_copy(ending.at[rows], fine_hbm.at[1, rows], piece_sem.at[k])
 
         def last(k, _):
             at = k * n
-            rise = slopes(act1, 1, at + HALO, n, HALO, cols_here)
-            for c in range(halves):
-                stage[1, pl.ds(at, n), :, halves_of(c)] = stage[0, pl.ds(at, n), :, halves_of(c)] + rise[c]
-            return 0
-
-        lax.fori_loop(0, rows_here // n, last, 0)
-        store(1, fine_hbm.at[1]).start()
-        store(2, coarse_hbm.at[0]).wait()
-        store(0, fine_hbm.at[0]).wait()
-        store(1, fine_hbm.at[1]).wait()
+            for a in range(3):
+                for b in range(3):
+                    for c in range(halves):
+                        window = act[c, pl.ds(at + HALO + a - 1, n), HALO + b : HALO + b + cols_here, :]
+                        patches[:, pl.ds((a * 3 + b) * channels + c * LANES, LANES)] = (
+                            window.reshape(m, LANES).astype(jnp.bfloat16)
+                        )
+            acc = jnp.dot(patches[...], w[...], preferred_element_type=jnp.float32)
+            ending[pl.ds(at, n)] = stage[0, pl.ds(at, n)] + step_size * acc.reshape(n, cols_here, channels)
+            piece_store(k).start()
+            return 0
+
+        lax.fori_loop(0, pieces, last, 0)
+        for k in range(pieces):
+            piece_store(k).wait()
+
+    coarse_store.wait()
+    first_store.wait()
 
 
 def two_sections(section_states, weights):
@@ -388,20 +417,20 @@
     most = max(largest_divisor(high - 2, 19), largest_divisor(high - 6, 17), largest_divisor(high - 4, 12))
     most_pixels = max(most * wide, largest_divisor(rows_here, 16) * cols_here)
     flat_weights = weights.reshape(2, 9 * channels, channels)
-    return pl.pallas_call(
+    any_space, in_vmem = pl.BlockSpec(memory_space=pl.ANY), pl.BlockSpec(memory_space=vmem)
+    act_last, w_last, stage = pl.pallas_call(
         functools.partial(cycle_kernel, sizes),
         out_shape=(
-            jax.ShapeDtypeStruct((2, rows_here, cols_here, channels), f32),
-            jax.ShapeDtypeStruct((1, rows_here, cols_here, channels), f32),
+            act,
+            vmem((9 * channels, channels), bf16),
+            vmem((3, rows_here, cols_here, channels), f32),
         ),
-        in_specs=[pl.BlockSpec(memory_space=pl.ANY)] * 2,
-        out_specs=[pl.BlockSpec(memory_space=pl.ANY)] * 2,
+        in_specs=[pl.BlockSpec(memory_space=pltpu.HBM)] * 2,
+        out_specs=[in_vmem] * 3,
         scratch_shapes=[
-            vmem((rows_here, cols_here, channels), f32),
-            vmem((2, 9 * channels, channels), bf16),
-            state, state, state, act, act,
+            vmem((9 * channels, channels), bf16),
+            state, state, state, act,
             vmem((-(-most_pixels // 16) * 16, 9 * channels), bf16),
-            vmem((3, rows_here, cols_here, channels), f32),
             vmem((2, halves, rows_here * HALO, LANES), f32),
             vmem((2, HALO * cols_here, channels), bf16),
             vmem((2, rows_here * HALO, channels), bf16),
@@ -409,14 +438,35 @@
             vmem((2, rows_here * HALO, channels), bf16),
             vmem((2, 2, HALO * HALO, channels), bf16),
             pltpu.SemaphoreType.DMA((3,)),
-            pltpu.SemaphoreType.DMA((3,)),
             pltpu.SemaphoreType.DMA((8,)),
             pltpu.SemaphoreType.DMA((8,)),
             pltpu.SemaphoreType.DMA((pieces,)),
             pltpu.SemaphoreType.DMA((pieces,)),
         ],
-        compiler_params=pltpu.CompilerParams(collective_id=0, has_side_effects=True),
-    )(section_states, flat_weights)
+        compiler_params=pltpu.CompilerParams(
+            collective_id=0, has_side_effects=True, vmem_limit_bytes=LIMIT
+        ),
+    )(
+        pltpu.with_memory_space_constraint(section_states, pltpu.HBM),
+        pltpu.with_memory_space_constraint(flat_weights, pltpu.HBM),
+    )
+    last_pieces = rows_here // largest_divisor(rows_here, 8)
+    return pl.pallas_call(
+        functools.partial(last_kernel, sizes[2]),
+        out_shape=(
+            jax.ShapeDtypeStruct((2, rows_here, cols_here, channels), f32),
+            jax.ShapeDtypeStruct((1, rows_here, cols_here, channels), f32),
+        ),
+        in_specs=[in_vmem] * 3,
+        out_specs=[any_space] * 2,
+        scratch_shapes=[
+            vmem((rows_here // last_pieces * cols_here, 9 * channels), bf16),
+            vmem((rows_here, cols_here, channels), f32),
+            pltpu.SemaphoreType.DMA((3,)),
+            pltpu.SemaphoreType.DMA((last_pieces,)),
+        ],
+        compiler_params=pltpu.CompilerParams(vmem_limit_bytes=LIMIT),
+    )(act_last, w_last, stage)
 
 
 def on_device(section_states, weights):

time: 20.9 us -> 18.1 us (0.87)
  local copies, waits for them, and re-layouts: 3.12 us -> 0 us
  Pallas kernels: 17 us -> 17.3 us
    unnamed x4 -> x0, local copies, waits for them, and re-layouts: 3.12 us -> none
    pallas_call x1 -> x2, Pallas kernels: 17 us -> 17.3 us  [the longest x1 15.1 us: two_sections(): pl.pallas_call(functools.partial(cycle_kernel, sizes), out_shape=(act, vm...]
where the time goes in v2:
time: 18.1 us; the launch traced here: 18 us
  Pallas kernels  17.3 us (96%)
  between operations  0.64 us (4%)
    pallas_call x1, Pallas kernels, two_sections(): pl.pallas_call(functools.partial(cycle_kernel, sizes), out_shape=(act, vm...  15.1 us
    pallas_call x1, Pallas kernels, two_sections(): pl.pallas_call(functools.partial(last_kernel, sizes[2]), out_shape=(jax.S...  2.21 us

profile of v2, /device:TPU:1, one launch (start us, length us, event | category | flops | bytes accessed | tf_op | source)
XLA Modules:
  0.0 18.0 jit_solution(5627439173016519438)
XLA Ops:
  0.6 15.1 %shard_map.41 = (f32[2,40,32,128]{3,2,1,0:T(8,128)S(1)}, bf16[2304,256]{1,0:T(8,128)(2,1)S(1)}, f32[3,32,16,256]{3,2,1,0:T(8,128)S(1)}) custom-call(f32[1,32,16,256]{3,2,1,0:T(8,128)} %x_hbm.1, bf16[2,2304,256]{2,1,0:T(8,128)(2,1)} %bitcast.1), custom_call_target="tpu_custom_call" | custom-call | tf_op jit(solution)/shard_map/pallas_call | solution.py:421
  15.8 2.2 %shard_map.42 = (f32[2,32,16,256]{3,2,1,0:T(8,128)}, f32[1,32,16,256]{3,2,1,0:T(8,128)}) custom-call(f32[2,40,32,128]{3,2,1,0:T(8,128)S(1)} %get-tuple-element.5.act, bf16[2304,256]{1,0:T(8,128)(2,1)S(1)} %get-tuple-element.6.w, f32[3,32,16,256]{3,2,1,0:T(8,128)S(1)} %get-tuple-element.7.stage), custom_call_target="tpu_custom_call" | custom-call | tf_op jit(solution)/shard_map/pallas_call | solution.py:454

commit v3 on v2

--- a/solution.py
+++ b/solution.py
@@ -110,7 +110,7 @@
 
 def cycle_kernel(
     sizes, x_hbm, w_hbm, act1, w_last, stage,
-    w_first, base, mid, end, act0, patches,
+    w_first, base, mid, end, act0, inside, patches,
     flat, send_row, send_col, recv_row, recv_col, recv_corner,
     load_sem, send_sem, recv_sem, pass_send, pass_recv,
 ):
@@ -152,23 +152,34 @@
     def halves_of(c):
         return pl.ds(c * LANES, LANES)
 
+    def silu(u):
+        half = 0.5 * u
+        return half + half * jnp.tanh(half)
+
     def masked_silu(u, first_row):
-        n = u.shape[0]
-        i = first_row + lax.broadcasted_iota(jnp.int32, (n, wide, LANES), 0) + (row * rows_here - HALO)
-        j = lax.broadcasted_iota(jnp.int32, (n, wide, LANES), 1) + (col * cols_here - HALO)
-        inside = (i >= 0) & (i < nrows * rows_here) & (j >= 0) & (j < ncols * cols_here)
-        return jnp.where(inside, u / (1.0 + jnp.exp(-u)), 0.0)
-
-    def slopes(act, layer, first_row, n, left, width):
-        m = n * width
+        half = 0.5 * u
+        kept = half * inside[pl.ds(first_row, u.shape[0])]
+        return kept + kept * jnp.tanh(half)
+
+    def mark_inside(k, _):
+        i = lax.broadcasted_iota(jnp.int32, (1, wide, LANES), 0) + (row * rows_here - HALO + k)
+        j = lax.broadcasted_iota(jnp.int32, (1, wide, LANES), 1) + (col * cols_here - HALO)
+        held = (i >= 0) & (i < nrows * rows_here) & (j >= 0) & (j < ncols * cols_here)
+        inside[pl.ds(k, 1)] = jnp.where(held, 1.0, 0.0)
+        return 0
+
+    lax.fori_loop(0, high, mark_inside, 0, unroll=4)
+
+    def slopes(act, layer, first_row, n, slot):
+        m, width, left = n * wide, wide, 0
         for a in range(3):
             for b in range(3):
                 for c in range(halves):
                     window = act[c, pl.ds(first_row + a - 1, n), left + b : left + b + width, :]
-                    patches[0:m, pl.ds((a * 3 + b) * channels + c * LANES, LANES)] = (
+                    patches[slot, 0:m, pl.ds((a * 3 + b) * channels + c * LANES, LANES)] = (
                         window.reshape(m, LANES).astype(jnp.bfloat16)
                     )
-        acc = jnp.dot(patches[0:m, :], w[layer][...], preferred_element_type=jnp.float32)
+        acc = jnp.dot(patches[slot, 0:m, :], w[layer][...], preferred_element_type=jnp.float32)
         return [
             step_size * acc[:, c * LANES : (c + 1) * LANES].reshape(n, width, LANES)
             for c in range(halves)
@@ -183,7 +194,7 @@
         lax.fori_loop(0, rows_here, body, 0, unroll=4)
 
     end_rows = high - 4
-    piece = largest_divisor(end_rows, 12)
+    piece = largest_divisor(end_rows, 9)
     pieces = end_rows // piece
 
     def hand_over(k):
@@ -194,22 +205,33 @@
             device_id=(1 - depth, row, col), device_id_type=MESH,
         )
 
-    def first_layer(source, target, first_row, total, limit):
+    def first_layer(source, target, first_row, total, limit, unrolled):
         n = largest_divisor(total, limit)
 
         def body(k, _):
             at = first_row + k * n
-            rise = slopes(act0, 0, at, n, 0, wide)
+            rise = slopes(act0, 0, at, n, k % 2 if unrolled else 0)
             for c in range(halves):
                 u = source[c, pl.ds(at, n)] + rise[c]
                 target[c, pl.ds(at, n)] = u
                 act1[c, pl.ds(at, n), 1 : 1 + wide, :] = masked_silu(u, at)
             return 0
 
-        lax.fori_loop(0, total // n, body, 0)
+        if unrolled:
+            for k in range(total // n):
+                body(k, 0)
+        else:
+            lax.fori_loop(0, total // n, body, 0)
 
     @pl.when(depth == 0)
     def _():
+        def clear(i, _):
+            for c in range(halves):
+                base[c, pl.ds(i, 1)] = jnp.zeros((1, wide, LANES), jnp.float32)
+                act0[c, pl.ds(i, 1)] = jnp.zeros((1,) + act0.shape[2:], jnp.float32)
+            return 0
+
+        lax.fori_loop(0, high, clear, 0, unroll=4)
         x_load.wait()
         for side in range(2):
             rows_from = 0 if side == 0 else rows_here - HALO
@@ -268,51 +290,53 @@
 
         def place(i, _):
             for c in range(halves):
-                base[c, i + HALO, HALO : HALO + cols_here, :] = x[i, :, halves_of(c)]
+                u = x[i, :, halves_of(c)]
+                base[c, i + HALO, HALO : HALO + cols_here, :] = u
+                act0[c, i + HALO, HALO + 1 : HALO + 1 + cols_here, :] = silu(u)
             return 0
 
         lax.fori_loop(0, rows_here, place, 0, unroll=4)
 
-        for exists, copy, arrival in copies:
+        def put(c, i, j, u, act):
+            base[c, i, j : j + u.shape[0], :] = u
+            act0[c, i, j + 1 : j + 1 + u.shape[0], :] = act
+
+        for k in (2, 3, 0, 1, 4, 5, 6, 7):
+            exists, copy, arrival = copies[k]
+            dr, dc = DIRECTIONS[k]
 
             @pl.when(exists)
-            def _(copy=copy, arrival=arrival):
+            def _(arrival=arrival, dr=dr, dc=dc):
                 arrival.wait_recv()
-
-        for side in range(2):
-            top = 0 if side == 0 else high - HALO
-            left = 0 if side == 0 else wide - HALO
-            for c in range(halves):
-                base[c, top : top + HALO, HALO : HALO + cols_here, :] = (
-                    recv_row[side, :, halves_of(c)].astype(jnp.float32).reshape(HALO, cols_here, LANES)
-                )
-                flat[side, c] = recv_col[side, :, halves_of(c)].astype(jnp.float32)
-                for i in range(rows_here):
-                    base[c, HALO + i, left : left + HALO, :] = flat[side, c, i * HALO : (i + 1) * HALO, :]
-            for other in range(2):
-                beside = 0 if other == 0 else wide - HALO
+                top = {-1: 0, 0: HALO, 1: high - HALO}[dr]
+                left = {-1: 0, 0: HALO, 1: wide - HALO}[dc]
                 for c in range(halves):
-                    block = recv_corner[side, other, :, halves_of(c)].astype(jnp.float32)
+                    if dr == 0:
+                        side = (dc + 1) // 2
+                        u = recv_col[side, :, halves_of(c)].astype(jnp.float32)
+                        flat[0, c] = u
+                        flat[1, c] = silu(u)
+                        for i in range(rows_here):
+                            part = slice(i * HALO, (i + 1) * HALO)
+                            put(c, top + i, left, flat[0, c, part, :], flat[1, c, part, :])
+                        continue
+                    if dc == 0:
+                        u = recv_row[(dr + 1) // 2, :, halves_of(c)].astype(jnp.float32)
+                    else:
+                        u = recv_corner[(dr + 1) // 2, (dc + 1) // 2, :, halves_of(c)].astype(jnp.float32)
+                    act, n = silu(u), u.shape[0] // HALO
                     for i in range(HALO):
-                        base[c, top + i, beside : beside + HALO, :] = block[i * HALO : (i + 1) * HALO]
-
-        n = largest_divisor(high, 8)
-
-        def start_act(k, _):
-            for c in range(halves):
-                u = base[c, pl.ds(k * n, n)]
-                act0[c, pl.ds(k * n, n), 1 : 1 + wide, :] = masked_silu(u, k * n)
-            return 0
-
-        lax.fori_loop(0, high // n, start_act, 0)
+                        part = slice(i * n, (i + 1) * n)
+                        put(c, top + i, left, u[part], act[part])
+
         w_loads[0].wait()
-        first_layer(base, mid, 1, high - 2, 19)
+        first_layer(base, mid, 1, high - 2, 19, False)
         stage_interior(mid, 0)
         w_loads[1].wait()
 
         def second(k, _):
             at = 2 + k * piece
-            rise = slopes(act1, 1, at, piece, 0, wide)
+            rise = slopes(act1, 1, at, piece, 0)
             for c in range(halves):
                 end[c, pl.ds(at, piece)] = mid[c, pl.ds(at, piece)] + rise[c]
             hand_over(k).start()
@@ -347,7 +371,7 @@
         lax.fori_loop(0, pieces, received, 0)
         stage_interior(end, 2)
         w_loads[0].wait()
-        first_layer(end, mid, 3, high - 6, 17)
+        first_layer(end, mid, 3, high - 6, 17, True)
         stage_interior(mid, 0)
         w_loads[1].wait()
 
@@ -382,21 +406,21 @@
             rows = pl.ds(k * n, n)
             return pltpu.make_async_copy(ending.at[rows], fine_hbm.at[1, rows], piece_sem.at[k])
 
-        def last(k, _):
+        def last(k):
             at = k * n
             for a in range(3):
                 for b in range(3):
                     for c in range(halves):
                         window = act[c, pl.ds(at + HALO + a - 1, n), HALO + b : HALO + b + cols_here, :]
-                        patches[:, pl.ds((a * 3 + b) * channels + c * LANES, LANES)] = (
+                        patches[k % 2, :, pl.ds((a * 3 + b) * channels + c * LANES, LANES)] = (
                             window.reshape(m, LANES).astype(jnp.bfloat16)
                         )
-            acc = jnp.dot(patches[...], w[...], preferred_element_type=jnp.float32)
+            acc = jnp.dot(patches[k % 2], w[...], preferred_element_type=jnp.float32)
             ending[pl.ds(at, n)] = stage[0, pl.ds(at, n)] + step_size * acc.reshape(n, cols_here, channels)
             piece_store(k).start()
-            return 0
-
-        lax.fori_loop(0, pieces, last, 0)
+
+        for k in range(pieces):
+            last(k)
         for k in range(pieces):
             piece_store(k).wait()
 
@@ -409,13 +433,13 @@
     halves = channels // LANES
     high, wide = rows_here + 2 * HALO, cols_here + 2 * HALO
     act_wide = -(-(wide + 2) // 8) * 8
-    pieces = (high - 4) // largest_divisor(high - 4, 12)
+    pieces = (high - 4) // largest_divisor(high - 4, 9)
     sizes = (lax.axis_size("rows"), lax.axis_size("cols"), 2.0 / (2 * lax.axis_size("depth")))
     f32, bf16, vmem = jnp.float32, jnp.bfloat16, pltpu.VMEM
     state = vmem((halves, high, wide, LANES), f32)
     act = vmem((halves, high, act_wide, LANES), f32)
-    most = max(largest_divisor(high - 2, 19), largest_divisor(high - 6, 17), largest_divisor(high - 4, 12))
-    most_pixels = max(most * wide, largest_divisor(rows_here, 16) * cols_here)
+    most = max(largest_divisor(high - 2, 19), largest_divisor(high - 6, 17), largest_divisor(high - 4, 9))
+    most_pixels = most * wide
     flat_weights = weights.reshape(2, 9 * channels, channels)
     any_space, in_vmem = pl.BlockSpec(memory_space=pl.ANY), pl.BlockSpec(memory_space=vmem)
     act_last, w_last, stage = pl.pallas_call(
@@ -430,7 +454,8 @@
         scratch_shapes=[
             vmem((9 * channels, channels), bf16),
             state, state, state, act,
-            vmem((-(-most_pixels // 16) * 16, 9 * channels), bf16),
+            vmem((high, wide, LANES), f32),
+            vmem((2, -(-most_pixels // 16) * 16, 9 * channels), bf16),
             vmem((2, halves, rows_here * HALO, LANES), f32),
             vmem((2, HALO * cols_here, channels), bf16),
             vmem((2, rows_here * HALO, channels), bf16),
@@ -460,7 +485,7 @@
         in_specs=[in_vmem] * 3,
         out_specs=[any_space] * 2,
         scratch_shapes=[
-            vmem((rows_here // last_pieces * cols_here, 9 * channels), bf16),
+            vmem((2, rows_here // last_pieces * cols_here, 9 * channels), bf16),
             vmem((rows_here, cols_here, channels), f32),
             pltpu.SemaphoreType.DMA((3,)),
             pltpu.SemaphoreType.DMA((last_pieces,)),

time: 18.1 us -> 17.1 us (0.945)
  Pallas kernels: 17.3 us -> 16.4 us
    pallas_call x1, Pallas kernels: 15.1 us -> 14.5 us  [two_sections(): pl.pallas_call(functools.partial(cycle_kernel, sizes), out_shape=(act, vm...]
    pallas_call x1, Pallas kernels: 2.21 us -> 1.86 us  [two_sections(): pl.pallas_call(functools.partial(last_kernel, sizes[2]), out_shape=(jax.S...]
where the time goes in v3:
time: 17.1 us; the launch traced here: 17 us
  Pallas kernels  16.4 us (96%)
  between operations  0.64 us (4%)
    pallas_call x1, Pallas kernels, two_sections(): pl.pallas_call(functools.partial(cycle_kernel, sizes), out_shape=(act, vm...  14.5 us
    pallas_call x1, Pallas kernels, two_sections(): pl.pallas_call(functools.partial(last_kernel, sizes[2]), out_shape=(jax.S...  1.86 us

profile of v3, /device:TPU:1, one launch (start us, length us, event | category | flops | bytes accessed | tf_op | source)
XLA Modules:
  0.0 17.0 jit_solution(16881479358176463717)
XLA Ops:
  0.6 14.5 %shard_map.41 = (f32[2,40,32,128]{3,2,1,0:T(8,128)S(1)}, bf16[2304,256]{1,0:T(8,128)(2,1)S(1)}, f32[3,32,16,256]{3,2,1,0:T(8,128)S(1)}) custom-call(f32[1,32,16,256]{3,2,1,0:T(8,128)} %x_hbm.1, bf16[2,2304,256]{2,1,0:T(8,128)(2,1)} %bitcast.1), custom_call_target="tpu_custom_call" | custom-call | tf_op jit(solution)/shard_map/pallas_call | solution.py:445
  15.1 1.9 %shard_map.42 = (f32[2,32,16,256]{3,2,1,0:T(8,128)}, f32[1,32,16,256]{3,2,1,0:T(8,128)}) custom-call(f32[2,40,32,128]{3,2,1,0:T(8,128)S(1)} %get-tuple-element.5.act, bf16[2304,256]{1,0:T(8,128)(2,1)S(1)} %get-tuple-element.6.w, f32[3,32,16,256]{3,2,1,0:T(8,128)S(1)} %get-tuple-element.7.stage), custom_call_target="tpu_custom_call" | custom-call | tf_op jit(solution)/shard_map/pallas_call | solution.py:479

commit v4 on v3

--- a/solution.py
+++ b/solution.py
@@ -170,20 +170,28 @@
 
     lax.fori_loop(0, high, mark_inside, 0, unroll=4)
 
-    def slopes(act, layer, first_row, n, slot):
-        m, width, left = n * wide, wide, 0
+    def slopes(act, layer, groups):
+        m = sum(n for _, n in groups) * wide
         for a in range(3):
             for b in range(3):
                 for c in range(halves):
-                    window = act[c, pl.ds(first_row + a - 1, n), left + b : left + b + width, :]
-                    patches[slot, 0:m, pl.ds((a * 3 + b) * channels + c * LANES, LANES)] = (
-                        window.reshape(m, LANES).astype(jnp.bfloat16)
-                    )
-        acc = jnp.dot(patches[slot, 0:m, :], w[layer][...], preferred_element_type=jnp.float32)
-        return [
-            step_size * acc[:, c * LANES : (c + 1) * LANES].reshape(n, width, LANES)
-            for c in range(halves)
-        ]
+                    filled = 0
+                    for first_row, n in groups:
+                        window = act[c, pl.ds(first_row + a - 1, n), b : b + wide, :]
+                        patches[filled : filled + n * wide, pl.ds((a * 3 + b) * channels + c * LANES, LANES)] = (
+                            window.reshape(n * wide, LANES).astype(jnp.bfloat16)
+                        )
+                        filled += n * wide
+        acc = jnp.dot(patches[0:m, :], w[layer][...], preferred_element_type=jnp.float32)
+        rises = []
+        filled = 0
+        for _, n in groups:
+            rise = step_size * acc[filled : filled + n * wide]
+            rises.append(
+                [rise[:, c * LANES : (c + 1) * LANES].reshape(n, wide, LANES) for c in range(halves)]
+            )
+            filled += n * wide
+        return rises
 
     def stage_interior(state, slot):
         def body(i, _):
@@ -205,23 +213,12 @@
             device_id=(1 - depth, row, col), device_id_type=MESH,
         )
 
-    def first_layer(source, target, first_row, total, limit, unrolled):
-        n = largest_divisor(total, limit)
-
-        def body(k, _):
-            at = first_row + k * n
-            rise = slopes(act0, 0, at, n, k % 2 if unrolled else 0)
+    def first_layer(source, groups):
+        for (at, n), rise in zip(groups, slopes(act0, 0, groups)):
             for c in range(halves):
                 u = source[c, pl.ds(at, n)] + rise[c]
-                target[c, pl.ds(at, n)] = u
+                mid[c, pl.ds(at, n)] = u
                 act1[c, pl.ds(at, n), 1 : 1 + wide, :] = masked_silu(u, at)
-            return 0
-
-        if unrolled:
-            for k in range(total // n):
-                body(k, 0)
-        else:
-            lax.fori_loop(0, total // n, body, 0)
 
     @pl.when(depth == 0)
     def _():
@@ -301,7 +298,7 @@
             base[c, i, j : j + u.shape[0], :] = u
             act0[c, i, j + 1 : j + 1 + u.shape[0], :] = act
 
-        for k in (2, 3, 0, 1, 4, 5, 6, 7):
+        def take(k):
             exists, copy, arrival = copies[k]
             dr, dc = DIRECTIONS[k]
 
@@ -330,13 +327,25 @@
                         put(c, top + i, left, u[part], act[part])
 
         w_loads[0].wait()
-        first_layer(base, mid, 1, high - 2, 19, False)
+        take(2)
+        take(3)
+        inner = rows_here - 2
+        step = largest_divisor(inner, 15)
+
+        def inner_rows(k, _):
+            first_layer(base, [(HALO + 1 + k * step, step)])
+            return 0
+
+        lax.fori_loop(0, inner // step, inner_rows, 0)
+        for k in (0, 1, 4, 5, 6, 7):
+            take(k)
+        first_layer(base, [(1, HALO), (high - HALO - 1, HALO)])
         stage_interior(mid, 0)
         w_loads[1].wait()
 
         def second(k, _):
             at = 2 + k * piece
-            rise = slopes(act1, 1, at, piece, 0)
+            rise = slopes(act1, 1, [(at, piece)])[0]
             for c in range(halves):
                 end[c, pl.ds(at, piece)] = mid[c, pl.ds(at, piece)] + rise[c]
             hand_over(k).start()
@@ -360,18 +369,19 @@
     def _():
         pl.semaphore_wait(barrier, 1)
 
+        w_loads[0].wait()
+
         def received(k, _):
             hand_over(k).wait_recv()
             at = 2 + k * piece
             for c in range(halves):
                 u = end[c, pl.ds(at, piece)]
                 act0[c, pl.ds(at, piece), 1 : 1 + wide, :] = masked_silu(u, at)
+            first_layer(end, [(at - 1, piece)])
             return 0
 
         lax.fori_loop(0, pieces, received, 0)
         stage_interior(end, 2)
-        w_loads[0].wait()
-        first_layer(end, mid, 3, high - 6, 17, True)
         stage_interior(mid, 0)
         w_loads[1].wait()
 
@@ -438,7 +448,7 @@
     f32, bf16, vmem = jnp.float32, jnp.bfloat16, pltpu.VMEM
     state = vmem((halves, high, wide, LANES), f32)
     act = vmem((halves, high, act_wide, LANES), f32)
-    most = max(largest_divisor(high - 2, 19), largest_divisor(high - 6, 17), largest_divisor(high - 4, 9))
+    most = max(largest_divisor(rows_here - 2, 15), 2 * HALO, largest_divisor(high - 4, 9))
     most_pixels = most * wide
     flat_weights = weights.reshape(2, 9 * channels, channels)
     any_space, in_vmem = pl.BlockSpec(memory_space=pl.ANY), pl.BlockSpec(memory_space=vmem)
@@ -455,7 +465,7 @@
             vmem((9 * channels, channels), bf16),
             state, state, state, act,
             vmem((high, wide, LANES), f32),
-            vmem((2, -(-most_pixels // 16) * 16, 9 * channels), bf16),
+            vmem((-(-most_pixels // 16) * 16, 9 * channels), bf16),
             vmem((2, halves, rows_here * HALO, LANES), f32),
             vmem((2, HALO * cols_here, channels), bf16),
             vmem((2, rows_here * HALO, channels), bf16),

time: 17.1 us -> 16.7 us (0.977)
  Pallas kernels: 16.4 us -> 15.9 us
    pallas_call x1, Pallas kernels: 14.5 us -> 14.1 us  [two_sections(): pl.pallas_call(functools.partial(cycle_kernel, sizes), out_shape=(act, vm...]
where the time goes in v4:
time: 16.7 us; the launch traced here: 16.6 us
  Pallas kernels  15.9 us (95%)
  between operations  0.64 us (4%)
    pallas_call x1, Pallas kernels, two_sections(): pl.pallas_call(functools.partial(cycle_kernel, sizes), out_shape=(act, vm...  14.1 us
    pallas_call x1, Pallas kernels, two_sections(): pl.pallas_call(functools.partial(last_kernel, sizes[2]), out_shape=(jax.S...  1.86 us

profile of v4, /device:TPU:1, one launch (start us, length us, event | category | flops | bytes accessed | tf_op | source)
XLA Modules:
  0.0 16.6 jit_solution(13432048255490386227)
XLA Ops:
  0.6 14.1 %shard_map.41 = (f32[2,40,32,128]{3,2,1,0:T(8,128)S(1)}, bf16[2304,256]{1,0:T(8,128)(2,1)S(1)}, f32[3,32,16,256]{3,2,1,0:T(8,128)S(1)}) custom-call(f32[1,32,16,256]{3,2,1,0:T(8,128)} %x_hbm.1, bf16[2,2304,256]{2,1,0:T(8,128)(2,1)} %bitcast.1), custom_call_target="tpu_custom_call" | custom-call | tf_op jit(solution)/shard_map/pallas_call | solution.py:455
  14.7 1.9 %shard_map.42 = (f32[2,32,16,256]{3,2,1,0:T(8,128)}, f32[1,32,16,256]{3,2,1,0:T(8,128)}) custom-call(f32[2,40,32,128]{3,2,1,0:T(8,128)S(1)} %get-tuple-element.5.act, bf16[2304,256]{1,0:T(8,128)(2,1)S(1)} %get-tuple-element.6.w, f32[3,32,16,256]{3,2,1,0:T(8,128)S(1)} %get-tuple-element.7.stage), custom_call_target="tpu_custom_call" | custom-call | tf_op jit(solution)/shard_map/pallas_call | solution.py:489

commit v5 on v4

--- a/solution.py
+++ b/solution.py
@@ -110,7 +110,7 @@
 
 def cycle_kernel(
     sizes, x_hbm, w_hbm, act1, w_last, stage,
-    w_first, base, mid, end, act0, inside, patches,
+    w_first, base, mid, end, act0, inside,
     flat, send_row, send_col, recv_row, recv_col, recv_corner,
     load_sem, send_sem, recv_sem, pass_send, pass_recv,
 ):
@@ -171,18 +171,17 @@
     lax.fori_loop(0, high, mark_inside, 0, unroll=4)
 
     def slopes(act, layer, groups):
-        m = sum(n for _, n in groups) * wide
+        lhs = []
         for a in range(3):
             for b in range(3):
                 for c in range(halves):
-                    filled = 0
-                    for first_row, n in groups:
-                        window = act[c, pl.ds(first_row + a - 1, n), b : b + wide, :]
-                        patches[filled : filled + n * wide, pl.ds((a * 3 + b) * channels + c * LANES, LANES)] = (
-                            window.reshape(n * wide, LANES).astype(jnp.bfloat16)
-                        )
-                        filled += n * wide
-        acc = jnp.dot(patches[0:m, :], w[layer][...], preferred_element_type=jnp.float32)
+                    parts = [
+                        act[c, pl.ds(first_row + a - 1, n), b : b + wide, :]
+                        .reshape(n * wide, LANES).astype(jnp.bfloat16)
+                        for first_row, n in groups
+                    ]
+                    lhs.append(parts[0] if len(parts) == 1 else jnp.concatenate(parts, axis=0))
+        acc = jnp.dot(jnp.concatenate(lhs, axis=1), w[layer][...], preferred_element_type=jnp.float32)
         rises = []
         filled = 0
         for _, n in groups:
@@ -327,19 +326,9 @@
                         put(c, top + i, left, u[part], act[part])
 
         w_loads[0].wait()
-        take(2)
-        take(3)
-        inner = rows_here - 2
-        step = largest_divisor(inner, 15)
-
-        def inner_rows(k, _):
-            first_layer(base, [(HALO + 1 + k * step, step)])
-            return 0
-
-        lax.fori_loop(0, inner // step, inner_rows, 0)
-        for k in (0, 1, 4, 5, 6, 7):
+        for k in (2, 3, 0, 1, 4, 5, 6, 7):
             take(k)
-        first_layer(base, [(1, HALO), (high - HALO - 1, HALO)])
+        first_layer(base, [(1, high - 2)])
         stage_interior(mid, 0)
         w_loads[1].wait()
 
@@ -387,7 +376,7 @@
 
 
 def last_kernel(
-    step_size, act, w, stage, fine_hbm, coarse_hbm, patches, ending, store_sem, piece_sem
+    step_size, act, w, stage, fine_hbm, coarse_hbm, ending, store_sem, piece_sem
 ):
     _, rows_here, cols_here, channels = stage.shape
     halves = channels // LANES
@@ -418,14 +407,12 @@
 
         def last(k):
             at = k * n
-            for a in range(3):
-                for b in range(3):
-                    for c in range(halves):
-                        window = act[c, pl.ds(at + HALO + a - 1, n), HALO + b : HALO + b + cols_here, :]
-                        patches[k % 2, :, pl.ds((a * 3 + b) * channels + c * LANES, LANES)] = (
-                            window.reshape(m, LANES).astype(jnp.bfloat16)
-                        )
-            acc = jnp.dot(patches[k % 2], w[...], preferred_element_type=jnp.float32)
+            lhs = [
+                act[c, pl.ds(at + HALO + a - 1, n), HALO + b : HALO + b + cols_here, :]
+                .reshape(m, LANES).astype(jnp.bfloat16)
+                for a in range(3) for b in range(3) for c in range(halves)
+            ]
+            acc = jnp.dot(jnp.concatenate(lhs, axis=1), w[...], preferred_element_type=jnp.float32)
             ending[pl.ds(at, n)] = stage[0, pl.ds(at, n)] + step_size * acc.reshape(n, cols_here, channels)
             piece_store(k).start()
 
@@ -448,8 +435,6 @@
     f32, bf16, vmem = jnp.float32, jnp.bfloat16, pltpu.VMEM
     state = vmem((halves, high, wide, LANES), f32)
     act = vmem((halves, high, act_wide, LANES), f32)
-    most = max(largest_divisor(rows_here - 2, 15), 2 * HALO, largest_divisor(high - 4, 9))
-    most_pixels = most * wide
     flat_weights = weights.reshape(2, 9 * channels, channels)
     any_space, in_vmem = pl.BlockSpec(memory_space=pl.ANY), pl.BlockSpec(memory_space=vmem)
     act_last, w_last, stage = pl.pallas_call(
@@ -465,7 +450,6 @@
             vmem((9 * channels, channels), bf16),
             state, state, state, act,
             vmem((high, wide, LANES), f32),
-            vmem((-(-most_pixels // 16) * 16, 9 * channels), bf16),
             vmem((2, halves, rows_here * HALO, LANES), f32),
             vmem((2, HALO * cols_here, channels), bf16),
             vmem((2, rows_here * HALO, channels), bf16),
@@ -495,7 +479,6 @@
         in_specs=[in_vmem] * 3,
         out_specs=[any_space] * 2,
         scratch_shapes=[
-            vmem((2, rows_here // last_pieces * cols_here, 9 * channels), bf16),
             vmem((rows_here, cols_here, channels), f32),
             pltpu.SemaphoreType.DMA((3,)),
             pltpu.SemaphoreType.DMA((last_pieces,)),

time: 16.7 us -> 15.7 us (0.940)
  Pallas kernels: 15.9 us -> 14.9 us
    pallas_call x1, Pallas kernels: 14.1 us -> 13.3 us  [two_sections(): pl.pallas_call(functools.partial(cycle_kernel, sizes), out_shape=(act, vm...]
    pallas_call x1, Pallas kernels: 1.86 us -> 1.56 us  [two_sections(): pl.pallas_call(functools.partial(last_kernel, sizes[2]), out_shape=(jax.S...]
where the time goes in v5:
time: 15.7 us; the launch traced here: 15.5 us
  Pallas kernels  14.9 us (95%)
  between operations  0.64 us (4%)
    pallas_call x1, Pallas kernels, two_sections(): pl.pallas_call(functools.partial(cycle_kernel, sizes), out_shape=(act, vm...  13.3 us
    pallas_call x1, Pallas kernels, two_sections(): pl.pallas_call(functools.partial(last_kernel, sizes[2]), out_shape=(jax.S...  1.56 us

profile of v5, /device:TPU:1, one launch (start us, length us, event | category | flops | bytes accessed | tf_op | source)
XLA Modules:
  0.0 15.5 jit_solution(12884937142414031788)
XLA Ops:
  0.6 13.3 %shard_map.41 = (f32[2,40,32,128]{3,2,1,0:T(8,128)S(1)}, bf16[2304,256]{1,0:T(8,128)(2,1)S(1)}, f32[3,32,16,256]{3,2,1,0:T(8,128)S(1)}) custom-call(f32[1,32,16,256]{3,2,1,0:T(8,128)} %x_hbm.1, bf16[2,2304,256]{2,1,0:T(8,128)(2,1)} %bitcast.1), custom_call_target="tpu_custom_call" | custom-call | tf_op jit(solution)/shard_map/pallas_call | solution.py:440
  13.9 1.6 %shard_map.42 = (f32[2,32,16,256]{3,2,1,0:T(8,128)}, f32[1,32,16,256]{3,2,1,0:T(8,128)}) custom-call(f32[2,40,32,128]{3,2,1,0:T(8,128)S(1)} %get-tuple-element.5.act, bf16[2304,256]{1,0:T(8,128)(2,1)S(1)} %get-tuple-element.6.w, f32[3,32,16,256]{3,2,1,0:T(8,128)S(1)} %get-tuple-element.7.stage), custom_call_target="tpu_custom_call" | custom-call | tf_op jit(solution)/shard_map/pallas_call | solution.py:473

commit v6 on v5

--- a/solution.py
+++ b/solution.py
@@ -279,7 +279,7 @@
                 device_id=target, device_id_type=MESH,
             )
             copies.append((exists, copy, arrival))
-        order = (4, 5, 6, 7, 2, 3, 0, 1)
+        order = (2, 3, 4, 5, 6, 7, 0, 1)
         for k in order:
             exists, copy, arrival = copies[k]
             pl.when(exists)(copy.start)
@@ -326,10 +326,9 @@
                         put(c, top + i, left, u[part], act[part])
 
         w_loads[0].wait()
-        for k in (2, 3, 0, 1, 4, 5, 6, 7):
+        for k in (0, 1, 4, 5, 6, 7, 2, 3):
             take(k)
         first_layer(base, [(1, high - 2)])
-        stage_interior(mid, 0)
         w_loads[1].wait()
 
         def second(k, _):
@@ -341,6 +340,7 @@
             return 0
 
         lax.fori_loop(0, pieces, second, 0)
+        stage_interior(mid, 0)
         stage_interior(end, 1)
         for exists, copy, arrival in copies:
 

time: 15.7 us -> 16.4 us (1.045)
  Pallas kernels: 14.9 us -> 15.6 us
    pallas_call x1, Pallas kernels: 13.3 us -> 14 us  [two_sections(): pl.pallas_call(functools.partial(cycle_kernel, sizes), out_shape=(act, vm...]
where the time goes in v6:
time: 16.4 us; the launch traced here: 16.2 us
  Pallas kernels  15.6 us (95%)
  between operations  0.64 us (4%)
    pallas_call x1, Pallas kernels, two_sections(): pl.pallas_call(functools.partial(cycle_kernel, sizes), out_shape=(act, vm...  14 us
    pallas_call x1, Pallas kernels, two_sections(): pl.pallas_call(functools.partial(last_kernel, sizes[2]), out_shape=(jax.S...  1.56 us

profile of v6, /device:TPU:1, one launch (start us, length us, event | category | flops | bytes accessed | tf_op | source)
XLA Modules:
  0.0 16.2 jit_solution(5582148905392430155)
XLA Ops:
  0.6 14.0 %shard_map.41 = (f32[2,40,32,128]{3,2,1,0:T(8,128)S(1)}, bf16[2304,256]{1,0:T(8,128)(2,1)S(1)}, f32[3,32,16,256]{3,2,1,0:T(8,128)S(1)}) custom-call(f32[1,32,16,256]{3,2,1,0:T(8,128)} %x_hbm.1, bf16[2,2304,256]{2,1,0:T(8,128)(2,1)} %bitcast.1), custom_call_target="tpu_custom_call" | custom-call | tf_op jit(solution)/shard_map/pallas_call | solution.py:440
  14.7 1.6 %shard_map.42 = (f32[2,32,16,256]{3,2,1,0:T(8,128)}, f32[1,32,16,256]{3,2,1,0:T(8,128)}) custom-call(f32[2,40,32,128]{3,2,1,0:T(8,128)S(1)} %get-tuple-element.5.act, bf16[2304,256]{1,0:T(8,128)(2,1)S(1)} %get-tuple-element.6.w, f32[3,32,16,256]{3,2,1,0:T(8,128)S(1)} %get-tuple-element.7.stage), custom_call_target="tpu_custom_call" | custom-call | tf_op jit(solution)/shard_map/pallas_call | solution.py:473

commit v7 on v6

--- a/solution.py
+++ b/solution.py
@@ -279,7 +279,7 @@
                 device_id=target, device_id_type=MESH,
             )
             copies.append((exists, copy, arrival))
-        order = (2, 3, 4, 5, 6, 7, 0, 1)
+        order = (4, 5, 6, 7, 2, 3, 0, 1)
         for k in order:
             exists, copy, arrival = copies[k]
             pl.when(exists)(copy.start)

time: 16.4 us -> 15.7 us (0.957)
  Pallas kernels: 15.6 us -> 14.9 us
    pallas_call x1, Pallas kernels: 14 us -> 13.3 us  [two_sections(): pl.pallas_call(functools.partial(cycle_kernel, sizes), out_shape=(act, vm...]
where the time goes in v7:
time: 15.7 us; the launch traced here: 15.5 us
  Pallas kernels  14.9 us (95%)
  between operations  0.64 us (4%)
    pallas_call x1, Pallas kernels, two_sections(): pl.pallas_call(functools.partial(cycle_kernel, sizes), out_shape=(act, vm...  13.3 us
    pallas_call x1, Pallas kernels, two_sections(): pl.pallas_call(functools.partial(last_kernel, sizes[2]), out_shape=(jax.S...  1.56 us

profile of v7, /device:TPU:1, one launch (start us, length us, event | category | flops | bytes accessed | tf_op | source)
XLA Modules:
  0.0 15.5 jit_solution(17756915955257916583)
XLA Ops:
  0.6 13.3 %shard_map.41 = (f32[2,40,32,128]{3,2,1,0:T(8,128)S(1)}, bf16[2304,256]{1,0:T(8,128)(2,1)S(1)}, f32[3,32,16,256]{3,2,1,0:T(8,128)S(1)}) custom-call(f32[1,32,16,256]{3,2,1,0:T(8,128)} %x_hbm.1, bf16[2,2304,256]{2,1,0:T(8,128)(2,1)} %bitcast.1), custom_call_target="tpu_custom_call" | custom-call | tf_op jit(solution)/shard_map/pallas_call | solution.py:440
  14.0 1.6 %shard_map.42 = (f32[2,32,16,256]{3,2,1,0:T(8,128)}, f32[1,32,16,256]{3,2,1,0:T(8,128)}) custom-call(f32[2,40,32,128]{3,2,1,0:T(8,128)S(1)} %get-tuple-element.5.act, bf16[2304,256]{1,0:T(8,128)(2,1)S(1)} %get-tuple-element.6.w, f32[3,32,16,256]{3,2,1,0:T(8,128)S(1)} %get-tuple-element.7.stage), custom_call_target="tpu_custom_call" | custom-call | tf_op jit(solution)/shard_map/pallas_call | solution.py:473
